TPU v7x, 8 devices: a whole 2x2x1 slice. The times are simulated.
8 devices in a mesh: dp: 1 (over z), row: 2 (over y), col: 2 (over x), core: 2 (over core).
Axes of the slice: x: 2, y: 2, z: 1, core: 2. Of those that a mesh axis runs over, the one named last changes fastest.
Arguments:
- x: bfloat16 [2048, 896], P(('dp', 'row', 'col', 'core'))
- route_idx: int32 [2048, 8], P(('dp', 'row', 'col', 'core'))
- gates: float32 [2048, 8], P(('dp', 'row', 'col', 'core'))
- w1: bfloat16 [384, 896, 256], P(('row', 'col', 'core'))
- w3: bfloat16 [384, 896, 256], P(('row', 'col', 'core'))
- w2: bfloat16 [384, 256, 896], P(('row', 'col', 'core'))
- dy: bfloat16 [2048, 896], P(('dp', 'row', 'col', 'core'))
Outputs:
- output 1: bfloat16 [2048, 896], P(('dp', 'row', 'col', 'core'))
- output 2: bfloat16 [2048, 896], P(('dp', 'row', 'col', 'core'))
- output 3: float32 [2048, 8], P(('dp', 'row', 'col', 'core'))
- output 4: float32 [384, 896, 256], P(('dp', 'row', 'col', 'core'))
- output 5: float32 [384, 896, 256], P(('dp', 'row', 'col', 'core'))
- output 6: float32 [384, 256, 896], P(('dp', 'row', 'col', 'core'))
All inputs are finite; a program needn't handle non-finite values.
Results may differ from a plain program's by a relative error of at most 0.0104075.
Values are sent between devices in bfloat16 or wider.
A program may use at most 1 GiB of HBM per device.

v0:
```python
import jax
import jax.numpy as jnp
from jax import lax
from jax.sharding import PartitionSpec as P


def _cap(td, ne, top):
    s = ne // top
    return 2 * (top * (td // ne) + (td % ne + s - 1) // s) + 2


def _slot_rows(e, ne, cap):
    n = e.shape[0]
    order = jnp.argsort(e, stable=True)
    counts = jnp.zeros((ne,), jnp.int32).at[e].add(1)
    starts = jnp.cumsum(counts) - counts
    rank = jnp.zeros((n,), jnp.int32).at[order].set(jnp.arange(n, dtype=jnp.int32))
    return e * cap + rank - starts[e]


def _to_experts(buf, npd, el, cap, ax):
    d = buf.shape[-1]
    r = lax.all_to_all(buf.reshape(npd, el * cap, d), ax, 0, 0, tiled=True)
    return r.reshape(npd, el, cap, d).transpose(1, 0, 2, 3).reshape(el, npd * cap, d)


def _to_sources(z, npd, el, cap, ax):
    d = z.shape[-1]
    s = z.reshape(el, npd, cap, d).transpose(1, 0, 2, 3).reshape(npd, el * cap, d)
    return lax.all_to_all(s, ax, 0, 0, tiled=True).reshape(npd * el * cap, d)


def solution(mesh):
    ep = ('row', 'col', 'core')
    npd = mesh.shape['row'] * mesh.shape['col'] * mesh.shape['core']
    tspec = P(('dp',) + ep, None)
    wspec = P(ep, None, None)
    gspec = P(('dp',) + ep, None, None)
    f32 = jnp.float32
    bf = jnp.bfloat16

    def body(x, route_idx, gates, w1, w3, w2, dy):
        td, top = route_idx.shape
        el, dm, fh = w1.shape
        ne = el * npd
        cap = _cap(td, ne, top)
        n = td * top
        tok = jnp.arange(n, dtype=jnp.int32) // top
        rows = _slot_rows(route_idx.reshape(n), ne, cap)
        xs = jnp.zeros((ne * cap, dm), bf).at[rows].set(x[tok])
        xe = _to_experts(xs, npd, el, cap, ep)
        u = jnp.einsum('erd,edf->erf', xe, w1, preferred_element_type=f32).astype(bf)
        v = jnp.einsum('erd,edf->erf', xe, w3, preferred_element_type=f32).astype(bf)
        uf = u.astype(f32)
        vf = v.astype(f32)
        act = (jax.nn.silu(uf) * vf).astype(bf)
        o = jnp.einsum('erf,efd->erd', act, w2, preferred_element_type=f32).astype(bf)
        o_slot = _to_sources(o, npd, el, cap, ep)[rows].reshape(td, top, dm)
        y = jnp.sum(gates[:, :, None] * o_slot.astype(f32), axis=1).astype(bf)
        dgates = jnp.einsum('tjd,td->tj', o_slot, dy, preferred_element_type=f32)
        dq = (gates[:, :, None] * dy[:, None, :].astype(f32)).astype(bf).reshape(n, dm)
        de = _to_experts(jnp.zeros((ne * cap, dm), bf).at[rows].set(dq), npd, el, cap, ep)
        da = jnp.einsum('erd,efd->erf', de, w2, preferred_element_type=f32).astype(bf)
        dw2 = jnp.einsum('erf,erd->efd', act, de, preferred_element_type=f32)
        sg = jax.nn.sigmoid(uf)
        du = (da.astype(f32) * vf * sg * (1 + uf * (1 - sg))).astype(bf)
        dv = (da.astype(f32) * jax.nn.silu(uf)).astype(bf)
        dw1 = jnp.einsum('erd,erf->edf', xe, du, preferred_element_type=f32)
        dw3 = jnp.einsum('erd,erf->edf', xe, dv, preferred_element_type=f32)
        dxp = (jnp.einsum('erf,edf->erd', du, w1, preferred_element_type=f32) + jnp.einsum('erf,edf->erd', dv, w3, preferred_element_type=f32)).astype(bf)
        dxs = _to_sources(dxp, npd, el, cap, ep)[rows].reshape(td, top, dm)
        dx = jnp.sum(dxs.astype(f32), axis=1).astype(bf)
        return y, dx, dgates, dw1, dw3, dw2

    return jax.shard_map(body, mesh=mesh, in_specs=(tspec, tspec, tspec, wspec, wspec, wspec, tspec), out_specs=(tspec, tspec, tspec, gspec, gspec, gspec), check_vma=False)
```

profile of v0, /device:TPU:0, one launch (start us, length us, event | category | flops | bytes accessed | tf_op | source)
XLA Modules:
  0.0 541.6 jit_solution(13451588870250559589)
XLA Ops:
  1.8 14.7 %scatter_custom_fusion.1 = s32[384]{0:T(512)S(1)} fusion(s32[2048]{0:T(1024)S(1)} %bitcast.64, s32[2048]{0:T(1024)S(1)} %broadcast.107, s32[]{:T(128)} %constant.33.clone.1), kind=kCustom, calls=%fused_computation.69 | custom fusion | flops 2048 | bytes 1540 | tf_op jit(solution)/shard_map/scatter-add | solution.py:15
  17.1 5.0 sort.17
  22.2 13.2 %gather_fusion = s32[2048]{0:T(1024)S(1)} fusion(s32[384]{0:T(512)S(1)} %bitcast_subtract_fusion, s32[2048]{0:T(1024)S(1)} %broadcast_clamp_fusion.2), kind=kCustom, calls=%fused_computation | custom fusion | bytes 24576 | tf_op jit(solution)/shard_map/gather | solution.py:18
  35.4 8.3 %scatter_custom_fusion = s32[2048]{0:T(1024)S(1)} fusion(s32[2048]{0:T(1024)S(1)} %compare_select_fusion.3, s32[2048]{0:T(1024)S(1)} %iota.12, s32[]{:T(128)} %constant.33.clone.1), kind=kCustom, calls=%fused_computation.65 | custom fusion | bytes 8196 | tf_op jit(solution)/shard_map/scatter | solution.py:17
  44.3 29.0 %scatter_custom_fusion.2 = bf16[5376,896]{1,0:T(8,128)(2,1)} fusion(s32[2048]{0:T(1024)S(1)} %get-tuple-element.9, bf16[]{:T(256)} %constant.18.clone.1, bf16[256,896]{1,0:T(8,128)(2,1)S(1)} %copy-done, s32[2048]{0:T(1024)S(1)} %get-tuple-element.10), kind=kCustom, calls=%fused_computation.42 | custom fusion | bytes 9633794 | tf_op jit(solution)/shard_map/scatter | solution.py:50
  78.6 16.2 %scatter_custom_fusion.3 = bf16[5376,896]{1,0:T(8,128)(2,1)} fusion(s32[2048]{0:T(1024)S(1)} %get-tuple-element.9, bf16[]{:T(256)} %constant.18.clone.1, f32[256,896]{1,0:T(8,128)S(1)} %convert_element_type.58, f32[2048]{0:T(1024)S(1)} %mul.61), kind=kCustom, calls=%fused_computation.40 | custom fusion | flops 3670016 | bytes 10559490 | tf_op jit(solution)/shard_map/scatter | solution.py:62
  94.8 91.5 %all-to-all-done = bf16[8,672,896]{2,1,0:T(8,128)(2,1)} async-done(((bf16[8,672,896]{2,1,0:T(8,128)(2,1)}), bf16[8,672,896]{2,1,0:T(8,128)(2,1)}, u32[]{:S(2)}, u32[]{:S(2)}) %all-to-all-start) | async-done | bytes 9633824 | tf_op jit(solution)/shard_map/all_to_all | solution.py:23
  190.3 10.9 %copy.55 = bf16[8,672,896]{2,0,1:T(8,128)(2,1)} copy(bf16[8,672,896]{2,1,0:T(8,128)(2,1)} %all-to-all-done) | data formatting | bytes 19267584 | tf_op jit(solution)/shard_map/all_to_all | solution.py:23
  201.2 9.4 %copy.56 = bf16[48,8,14,896]{3,0,2,1:T(8,128)(2,1)} copy(bf16[48,8,14,896]{3,1,2,0:T(8,128)(2,1)} %bitcast.55) | data formatting | bytes 19267584 | tf_op jit(solution)/shard_map/transpose | solution.py:24
  210.6 14.6 %fusion.32 = bf16[48,112,256]{2,1,0:T(8,128)(2,1)} fusion(bf16[48,896,256]{2,1,0:T(8,128)(2,1)} %param.10, bf16[48,112,896]{2,0,1:T(8,128)(2,1)} %bitcast.47), kind=kOutput, calls=%fused_computation.50 | convolution fusion | flops 2467627008 | bytes 34406400 | tf_op jit(solution)/shard_map/erd,edf->erf/dot_general | solution.py:52
  225.2 12.1 %fusion.35 = bf16[48,112,256]{2,1,0:T(8,128)(2,1)} fusion(bf16[48,896,256]{2,1,0:T(8,128)(2,1)} %param.11, bf16[48,112,896]{2,0,1:T(8,128)(2,1)S(1)} %bitcast.50), kind=kOutput, calls=%fused_computation.51 | convolution fusion | flops 2467627008 | bytes 34406400 | tf_op jit(solution)/shard_map/erd,edf->erf/dot_general | solution.py:53
  237.3 15.2 %convolution_convert_fusion = bf16[48,112,896]{2,1,0:T(8,128)(2,1)} fusion(bf16[48,256,896]{2,1,0:T(8,128)(2,1)} %param.12, bf16[48,112,256]{2,1,0:T(8,128)(2,1)} %fusion.35, bf16[48,112,256]{2,1,0:T(8,128)(2,1)} %fusion.32), kind=kOutput, calls=%fused_computation.22 | convolution fusion | flops 2482077696 | bytes 37158912 | tf_op jit(solution)/shard_map/erf,efd->erd/dot_general | solution.py:57
  252.5 9.5 %copy.59 = bf16[48,112,896]{2,0,1:T(8,128)(2,1)} copy(bf16[48,112,896]{2,1,0:T(8,128)(2,1)} %convolution_convert_fusion) | data formatting | bytes 19267584 | tf_op jit(solution)/shard_map/convert_element_type | solution.py:57
  262.0 10.9 %copy.60 = bf16[8,48,14,896]{3,0,2,1:T(8,128)(2,1)} copy(bf16[8,48,14,896]{3,1,2,0:T(8,128)(2,1)} %bitcast.56) | data formatting | bytes 19267584 | tf_op jit(solution)/shard_map/transpose | solution.py:29
  273.0 8.8 %copy.61 = bf16[8,672,896]{2,1,0:T(8,128)(2,1)} copy(bf16[8,672,896]{2,0,1:T(8,128)(2,1)} %bitcast.57) | data formatting | bytes 19267584 | tf_op jit(solution)/shard_map/reshape | solution.py:29
  281.7 15.9 %all-to-all-done.2 = bf16[8,672,896]{2,1,0:T(8,128)(2,1)} async-done(((bf16[8,672,896]{2,1,0:T(8,128)(2,1)}), bf16[8,672,896]{2,1,0:T(8,128)(2,1)}, u32[]{:S(2)}, u32[]{:S(2)}) %all-to-all-start.2) | async-done | bytes 9633824 | tf_op jit(solution)/shard_map/all_to_all | solution.py:23
  301.8 10.9 %copy.63 = bf16[8,672,896]{2,0,1:T(8,128)(2,1)} copy(bf16[8,672,896]{2,1,0:T(8,128)(2,1)} %all-to-all-done.2) | data formatting | bytes 19267584 | tf_op jit(solution)/shard_map/all_to_all | solution.py:23
  312.8 9.5 %copy.64 = bf16[48,8,14,896]{3,0,2,1:T(8,128)(2,1)} copy(bf16[48,8,14,896]{3,1,2,0:T(8,128)(2,1)} %bitcast.58) | data formatting | bytes 19267584 | tf_op jit(solution)/shard_map/transpose | solution.py:24
  322.3 13.5 %fusion.38 = bf16[48,112,256]{2,1,0:T(8,128)(2,1)S(1)} fusion(bf16[48,256,896]{2,1,0:T(8,128)(2,1)} %param.12, bf16[48,112,896]{2,0,1:T(8,128)(2,1)} %bitcast.51), kind=kOutput, calls=%fused_computation.52 | convolution fusion | flops 2467627008 | bytes 34406400 | tf_op jit(solution)/shard_map/erd,efd->erf/dot_general | solution.py:63
  337.3 18.5 %fusion.51 = f32[48,112,896]{2,1,0:T(8,128)} fusion(bf16[48,896,256]{2,1,0:T(8,128)(2,1)} %param.10, bf16[48,112,256]{2,1,0:T(8,128)(2,1)} %fusion.35, bf16[48,112,256]{2,1,0:T(8,128)(2,1)S(1)} %fusion.38, bf16[48,112,256]{2,1,0:T(8,128)(2,1)S(1)} %copy-done.3), kind=kOutput, calls=%fused_computation.71 | convolution fusion | flops 2484142080 | bytes 49545216 | tf_op jit(solution)/shard_map/erf,edf->erd/dot_general | solution.py:70
  355.8 20.0 %add_convert_fusion = bf16[48,112,896]{2,1,0:T(8,128)(2,1)} fusion(f32[48,112,896]{2,1,0:T(8,128)} %fusion.51, bf16[48,896,256]{2,1,0:T(8,128)(2,1)} %param.11, bf16[48,112,256]{2,1,0:T(8,128)(2,1)} %copy-done.4, bf16[48,112,256]{2,1,0:T(8,128)(2,1)S(1)} %copy-done.3), kind=kOutput, calls=%fused_computation.8 | convolution fusion | flops 2486894592 | bytes 56426496 | tf_op jit(solution)/shard_map/erf,edf->erd/dot_general | solution.py:70
  375.8 9.5 %copy.66 = bf16[48,112,896]{2,0,1:T(8,128)(2,1)} copy(bf16[48,112,896]{2,1,0:T(8,128)(2,1)} %add_convert_fusion) | data formatting | bytes 19267584 | tf_op jit(solution)/shard_map/convert_element_type | solution.py:70
  385.3 10.8 %copy.67 = bf16[8,48,14,896]{3,0,2,1:T(8,128)(2,1)} copy(bf16[8,48,14,896]{3,1,2,0:T(8,128)(2,1)} %bitcast.59) | data formatting | bytes 19267584 | tf_op jit(solution)/shard_map/transpose | solution.py:29
  396.1 8.7 %copy.68 = bf16[8,672,896]{2,1,0:T(8,128)(2,1)} copy(bf16[8,672,896]{2,0,1:T(8,128)(2,1)} %bitcast.60) | data formatting | bytes 19267584 | tf_op jit(solution)/shard_map/reshape | solution.py:29
  413.2 20.3 %fusion = f32[48,256,896]{2,1,0:T(8,128)} fusion(bf16[48,112,896]{2,0,1:T(8,128)(2,1)} %bitcast.52, bf16[48,112,256]{2,1,0:T(8,128)(2,1)} %fusion.35, bf16[48,112,256]{2,1,0:T(8,128)(2,1)S(1)} %copy-done.3), kind=kOutput, calls=%fused_computation.9 | convolution fusion | flops 2477260800 | bytes 59179008 | tf_op jit(solution)/shard_map/erf,erd->efd/dot_general | solution.py:64
  433.5 19.0 %fusion.5 = f32[48,896,256]{2,1,0:T(8,128)} fusion(bf16[48,112,896]{2,0,1:T(8,128)(2,1)} %bitcast.48, bf16[48,112,256]{2,1,0:T(8,128)(2,1)S(1)} %copy-done.5, bf16[48,112,256]{2,1,0:T(8,128)(2,1)S(1)} %copy-done.3), kind=kOutput, calls=%fused_computation.23 | convolution fusion | flops 2477260800 | bytes 59179008 | tf_op jit(solution)/shard_map/erd,erf->edf/dot_general | solution.py:69
  452.5 19.6 %fusion.7 = f32[48,896,256]{2,1,0:T(8,128)} fusion(bf16[48,112,896]{2,0,1:T(8,128)(2,1)} %bitcast.49, bf16[48,112,256]{2,1,0:T(8,128)(2,1)} %fusion.35, bf16[48,112,256]{2,1,0:T(8,128)(2,1)S(1)} %copy-done.5, bf16[48,112,256]{2,1,0:T(8,128)(2,1)S(1)} %copy-done.3), kind=kOutput, calls=%fused_computation.25 | convolution fusion | flops 2484142080 | bytes 61931520 | tf_op jit(solution)/shard_map/erd,erf->edf/dot_general | solution.py:68
  472.1 15.7 %gather_fusion.1 = bf16[2048,896]{1,0:T(8,128)(2,1)} fusion(bf16[5376,896]{1,0:T(8,128)(2,1)} %bitcast.11, s32[2048]{0:T(1024)S(1)} %copy-done.10), kind=kCustom, calls=%fused_computation.2 | custom fusion | bytes 7348224 | tf_op jit(solution)/shard_map/gather | solution.py:58
  492.9 5.1 multiply_reduce_fusion
  498.0 22.6 %all-to-all-done.3 = bf16[8,672,896]{2,1,0:T(8,128)(2,1)} async-done(((bf16[8,672,896]{2,1,0:T(8,128)(2,1)}), bf16[8,672,896]{2,1,0:T(8,128)(2,1)}, u32[]{:S(2)}, u32[]{:S(2)}) %all-to-all-start.3) | async-done | bytes 9633824 | tf_op jit(solution)/shard_map/all_to_all | solution.py:30
  520.6 15.5 %gather_fusion.2 = bf16[2048,896]{1,0:T(8,128)(2,1)} fusion(bf16[5376,896]{1,0:T(8,128)(2,1)} %bitcast.21, s32[2048]{0:T(1024)S(1)} %copy-done.10), kind=kCustom, calls=%fused_computation.3 | custom fusion | bytes 7348224 | tf_op jit(solution)/shard_map/gather | solution.py:71
  536.1 5.3 bitcast_reduce_fusion
  (50 shorter events, 30.8 us)
Async XLA Ops:
  0.6 43.7 %copy-start = (bf16[256,896]{1,0:T(8,128)(2,1)S(1)}, bf16[256,896]{1,0:T(8,128)(2,1)}, u32[]{:S(2)}) copy-start(bf16[256,896]{1,0:T(8,128)(2,1)} %param.7) | copy-start | bytes 1376260
  73.3 4.9 copy-start.11
  73.3 5.2 copy-start.8
  73.3 113.0 %all-to-all-start = ((bf16[8,672,896]{2,1,0:T(8,128)(2,1)}), bf16[8,672,896]{2,1,0:T(8,128)(2,1)}, u32[]{:S(2)}, u32[]{:S(2)}) async-start(bf16[8,672,896]{2,1,0:T(8,128)(2,1)} %bitcast.54), calls=%async_computation | async-start | bytes 19267584 | tf_op jit(solution)/shard_map/all_to_all | solution.py:23
  78.4 16.4 %copy-start.6 = (f32[256,8]{1,0:T(8,128)}, f32[256,8]{1,0:T(8,128)S(1)}, u32[]{:S(2)}) copy-start(f32[256,8]{1,0:T(8,128)S(1)} %copy.52) | copy-start | bytes 24580
  186.3 111.3 %all-to-all-start.2 = ((bf16[8,672,896]{2,1,0:T(8,128)(2,1)}), bf16[8,672,896]{2,1,0:T(8,128)(2,1)}, u32[]{:S(2)}, u32[]{:S(2)}) async-start(bf16[8,672,896]{2,1,0:T(8,128)(2,1)} %bitcast.53), calls=%async_computation.2 | async-start | bytes 19267584 | tf_op jit(solution)/shard_map/all_to_all | solution.py:23
  210.6 14.6 %copy-start.2 = (bf16[48,8,14,896]{3,0,2,1:T(8,128)(2,1)S(1)}, bf16[48,8,14,896]{3,0,2,1:T(8,128)(2,1)}, u32[]{:S(2)}) copy-start(bf16[48,8,14,896]{3,0,2,1:T(8,128)(2,1)} %copy.56) | copy-start | bytes 28901380
  297.6 111.5 %all-to-all-start.1 = ((bf16[8,672,896]{2,1,0:T(8,128)(2,1)}), bf16[8,672,896]{2,1,0:T(8,128)(2,1)}, u32[]{:S(2)}, u32[]{:S(2)}) async-start(bf16[8,672,896]{2,1,0:T(8,128)(2,1)} %copy.61), calls=%async_computation.1 | async-start | bytes 19267584 | tf_op jit(solution)/shard_map/all_to_all | solution.py:30
  322.3 15.0 %copy-start.3 = (bf16[48,112,256]{2,1,0:T(8,128)(2,1)S(1)}, bf16[48,112,256]{2,1,0:T(8,128)(2,1)}, u32[]{:S(2)}) copy-start(bf16[48,112,256]{2,1,0:T(8,128)(2,1)} %fusion.32) | copy-start | bytes 8257540
  335.8 1.6 copy-start.4
  409.2 111.4 %all-to-all-start.3 = ((bf16[8,672,896]{2,1,0:T(8,128)(2,1)}), bf16[8,672,896]{2,1,0:T(8,128)(2,1)}, u32[]{:S(2)}, u32[]{:S(2)}) async-start(bf16[8,672,896]{2,1,0:T(8,128)(2,1)} %copy.68), calls=%async_computation.3 | async-start | bytes 19267584 | tf_op jit(solution)/shard_map/all_to_all | solution.py:30
  413.2 20.3 %copy-start.5 = (bf16[48,112,256]{2,1,0:T(8,128)(2,1)S(1)}, bf16[48,112,256]{2,1,0:T(8,128)(2,1)}, u32[]{:S(2)}) copy-start(bf16[48,112,256]{2,1,0:T(8,128)(2,1)} %copy-done.4) | copy-start | bytes 8257540
  452.5 19.6 %copy-start.10 = (s32[2048]{0:T(1024)S(1)}, s32[2048]{0:T(1024)}, u32[]{:S(2)}) copy-start(s32[2048]{0:T(1024)} %get-tuple-element.8) | copy-start | bytes 24580
  472.1 15.7 %copy-start.9 = (bf16[256,896]{1,0:T(8,128)(2,1)S(1)}, bf16[256,896]{1,0:T(8,128)(2,1)}, u32[]{:S(2)}) copy-start(bf16[256,896]{1,0:T(8,128)(2,1)} %param.13) | copy-start | bytes 1376260
  487.8 5.1 copy-start.7
  520.6 20.8 %copy-start.1 = (bf16[256,896]{1,0:T(8,128)(2,1)S(1)}, bf16[256,896]{1,0:T(8,128)(2,1)}, u32[]{:S(2)}) copy-start(bf16[256,896]{1,0:T(8,128)(2,1)} %param.7) | copy-start | bytes 1376260
where the time goes:
time: 546 us; the launch traced here: 542 us
  local copies, waits for them, and re-layouts  185 us (34%)
  matrix products  157 us (29%)
  waiting for transfers between devices  134 us (25%)
  other arithmetic  47.4 us (9%)
  starting transfers between devices  17.1 us (3%)
    all_to_all x2, waiting for transfers between devices, _to_experts(): r = lax.all_to_all(buf.reshape(npd, el * cap, d), ax, 0, 0, tiled=True)  107 us
    scatter x1, local copies, waits for them, and re-layouts, body(): xs = jnp.zeros((ne * cap, dm), bf).at[rows].set(x[tok])  29 us
    all_to_all x2, waiting for transfers between devices, _to_sources(): return lax.all_to_all(s, ax, 0, 0, tiled=True).reshape(npd * el * cap, d)  26.9 us
    all_to_all x2, local copies, waits for them, and re-layouts, _to_experts(): r = lax.all_to_all(buf.reshape(npd, el * cap, d), ax, 0, 0, tiled=True)  21.8 us
    transpose x2, local copies, waits for them, and re-layouts, _to_sources(): z.reshape(el, npd, cap, d).transpose(1, 0, 2, 3).reshape(npd, el * cap, d)  21.7 us
    dot_general x1, matrix products, body(): dw2 = jnp.einsum('erf,erd->efd', act, de, preferred_element_type=f32)  20.3 us
    dot_general x1, matrix products, body(): jnp.einsum('erf,edf->erd', dv, w3, preferred_element_type=f32)  20 us
    dot_general x1, matrix products, body(): dw1 = jnp.einsum('erd,erf->edf', xe, du, preferred_element_type=f32)  19.6 us
  transfers between devices with their start and end apart: 4, of which 4 were waited for; matrix products, arithmetic and copies ran while one was open for 54% of the time, Pallas kernels for 0%

commit v1 on v0

v1 whole, which is shorter than its diff:
```python
import functools

import jax
import jax.numpy as jnp
from jax import lax
from jax.experimental import pallas as pl
from jax.experimental.pallas import tpu as pltpu
from jax.sharding import PartitionSpec as P

F32 = jnp.float32
BF = jnp.bfloat16
CAP = 16
GRP = 16

_T00 = (((0,), (0,)), ((), ()))
_T11 = (((1,), (1,)), ((), ()))


def _dot(a, b, dims=(((1,), (0,)), ((), ()))):
    return lax.dot_general(a, b, dims, preferred_element_type=F32)


def _prep(aux, e0, s, td, el, pos_scr, gate_scr):
    top = aux.shape[0] // 2
    ei = lax.broadcasted_iota(jnp.int32, (el, td), 0).astype(F32)
    hit = jnp.zeros((el, td), F32)
    gate = jnp.zeros((el, td), F32)
    for j in range(top):
        eq = (aux[j:j + 1, :] - e0) == ei
        hit = jnp.where(eq, 1.0, hit)
        gate = jnp.where(eq, aux[top + j:top + j + 1, :], gate)
    before = lax.broadcasted_iota(jnp.int32, (td, td), 0) < lax.broadcasted_iota(jnp.int32, (td, td), 1)
    upper = jnp.where(before, 1.0, 0.0).astype(BF)
    rank = _dot(hit.astype(BF), upper)
    pos_scr[s] = jnp.where(hit > 0.0, rank, -1.0)
    if gate_scr is not None:
        gate_scr[s] = gate


def _mask(pos_scr, s, g, td):
    ci = lax.broadcasted_iota(jnp.int32, (CAP, td), 0).astype(F32)
    pg = pos_scr[s, pl.ds(pl.multiple_of(g * GRP, GRP), GRP), :]
    return jnp.concatenate([jnp.broadcast_to(pg[k:k + 1, :], (CAP, td)) == ci for k in range(GRP)], axis=0)


def _slot_gate(mask, gate_scr, s, g, td):
    gg = gate_scr[s, pl.ds(pl.multiple_of(g * GRP, GRP), GRP), :]
    rep = jnp.concatenate([jnp.broadcast_to(gg[k:k + 1, :], (CAP, td)) for k in range(GRP)], axis=0)
    return jnp.sum(jnp.where(mask, rep, 0.0), axis=1, keepdims=True)


def _onehot(mask):
    return jnp.where(mask, 1.0, 0.0).astype(BF)


def _e0(el):
    i = (lax.axis_index('row') * lax.axis_size('col') + lax.axis_index('col')) * lax.axis_size('core') + lax.axis_index('core')
    return (i * el).astype(F32)


def _fwd_kernel(npd, td, el, aux_ref, x_ref, w1_ref, w3_ref, w2_ref, y_ref, u_ref, v_ref, xe_ref, pos_scr, gate_scr, xg, og):
    i = pl.program_id(0)
    k = i % GRP
    g = i // GRP
    dm = x_ref.shape[1]

    @pl.when(i == 0)
    def _():
        def one(s, c):
            _prep(aux_ref[s], _e0(el), s, td, el, pos_scr, gate_scr)
            y_ref[pl.ds(pl.multiple_of(s * td, td), td), :] = jnp.zeros((td, dm), F32)
            return c
        lax.fori_loop(0, npd, one, 0)

    @pl.when(k == 0)
    def _():
        def one(s, c):
            m = _onehot(_mask(pos_scr, s, g, td))
            xs = x_ref[pl.ds(pl.multiple_of(s * td, td), td), :]
            xg[:, s] = _dot(m, xs).astype(BF).reshape(GRP, CAP, dm)
            return c
        lax.fori_loop(0, npd, one, 0)

    xe = xg[k].reshape(npd * CAP, dm)
    xe_ref[0] = xe
    u = _dot(xe, w1_ref[0]).astype(BF)
    v = _dot(xe, w3_ref[0]).astype(BF)
    u_ref[0] = u
    v_ref[0] = v
    uf = u.astype(F32)
    act = (uf * jax.nn.sigmoid(uf) * v.astype(F32)).astype(BF)
    og[k] = _dot(act, w2_ref[0]).astype(BF).reshape(npd, CAP, dm)

    @pl.when(k == GRP - 1)
    def _():
        def one(s, c):
            m = _mask(pos_scr, s, g, td)
            gs = _slot_gate(m, gate_scr, s, g, td)
            hi = gs.astype(BF).astype(F32)
            mid = (gs - hi).astype(BF).astype(F32)
            lo = gs - hi - mid
            os = og[:, s].reshape(GRP * CAP, dm)
            acc = _dot(jnp.where(m, hi, 0.0).astype(BF), os, _T00)
            acc += _dot(jnp.where(m, mid, 0.0).astype(BF), os, _T00)
            acc += _dot(jnp.where(m, lo, 0.0).astype(BF), os, _T00)
            y_ref[pl.ds(pl.multiple_of(s * td, td), td), :] += acc
            return c
        lax.fori_loop(0, npd, one, 0)


def _bwd_kernel(npd, td, el, aux_ref, dy_ref, u_ref, v_ref, w1_ref, w3_ref, w2_ref,
                dx_ref, dg_ref, dw2_ref, du_ref, dv_ref, pos_scr, gate_scr, dyg, pg, gsg, dgg):
    i = pl.program_id(0)
    k = i % GRP
    g = i // GRP
    dm = dy_ref.shape[1]
    top = dg_ref.shape[1]

    @pl.when(i == 0)
    def _():
        def one(s, c):
            _prep(aux_ref[s], _e0(el), s, td, el, pos_scr, gate_scr)
            dx_ref[pl.ds(pl.multiple_of(s * td, td), td), :] = jnp.zeros((td, dm), F32)
            dg_ref[s] = jnp.zeros((top, td), F32)
            return c
        lax.fori_loop(0, npd, one, 0)

    @pl.when(k == 0)
    def _():
        def one(s, c):
            m = _mask(pos_scr, s, g, td)
            gs = _slot_gate(m, gate_scr, s, g, td)
            gsg[:, s] = jnp.broadcast_to(gs, (GRP * CAP, 128)).reshape(GRP, CAP, 128)
            dys = dy_ref[pl.ds(pl.multiple_of(s * td, td), td), :]
            dyg[:, s] = _dot(_onehot(m), dys).astype(BF).reshape(GRP, CAP, dm)
            return c
        lax.fori_loop(0, npd, one, 0)

    rows = npd * CAP
    dye = dyg[k].reshape(rows, dm).astype(F32)
    gs = gsg[k].reshape(rows, 128)
    q = (jnp.concatenate([gs] * (dm // 128), axis=1) * dye).astype(BF)
    uf = u_ref[0].astype(F32)
    vf = v_ref[0].astype(F32)
    sg = jax.nn.sigmoid(uf)
    sl = uf * sg
    act = (sl * vf).astype(BF)
    w2 = w2_ref[0]
    o = _dot(act, w2).astype(BF).astype(F32)
    dgs = jnp.sum(dye * o, axis=1, keepdims=True)
    dgg[k] = jnp.broadcast_to(dgs, (rows, 128)).reshape(npd, CAP, 128)
    da = _dot(q, w2, _T11).astype(BF).astype(F32)
    dw2_ref[0] = _dot(act, q, _T00)
    du = (da * vf * sg * (1 + uf * (1 - sg))).astype(BF)
    dv = (da * sl).astype(BF)
    du_ref[0] = du
    dv_ref[0] = dv
    p = _dot(du, w1_ref[0], _T11) + _dot(dv, w3_ref[0], _T11)
    pg[k] = p.astype(BF).reshape(npd, CAP, dm)

    @pl.when(k == GRP - 1)
    def _():
        def one(s, c):
            m = _mask(pos_scr, s, g, td)
            ps = pg[:, s].reshape(GRP * CAP, dm)
            dx_ref[pl.ds(pl.multiple_of(s * td, td), td), :] += _dot(_onehot(m), ps, _T00)
            dgr = dgg[:, s].reshape(GRP * CAP, 128)
            dgr = jnp.concatenate([dgr] * (td // 128), axis=1)
            dge = jnp.sum(jnp.where(m, dgr, 0.0).reshape(GRP, CAP, td), axis=1)
            ei = (lax.broadcasted_iota(jnp.int32, (GRP, td), 0) + g * GRP).astype(F32)
            aux = aux_ref[s]
            e0 = _e0(el)
            out = [jnp.sum(jnp.where((aux[j:j + 1, :] - e0) == ei, dge, 0.0), axis=0, keepdims=True) for j in range(top)]
            dg_ref[s] += jnp.concatenate(out, axis=0)
            return c
        lax.fori_loop(0, npd, one, 0)


def _dw_kernel(xe_ref, du_ref, dv_ref, dw1_ref, dw3_ref):
    xe = xe_ref[0]
    dw1_ref[0] = _dot(xe, du_ref[0], _T00)
    dw3_ref[0] = _dot(xe, dv_ref[0], _T00)


def _full(shape):
    n = len(shape)
    return pl.BlockSpec(shape, lambda i: (0,) * n, pipeline_mode=pl.Buffered(1))


def _per(shape):
    n = len(shape)
    return pl.BlockSpec((1,) + shape, lambda i: (i,) + (0,) * n)


def solution(mesh):
    ep = ('row', 'col', 'core')
    npd = mesh.shape['row'] * mesh.shape['col'] * mesh.shape['core']
    tspec = P(('dp',) + ep, None)
    wspec = P(ep, None, None)
    gspec = P(('dp',) + ep, None, None)

    def body(x, route_idx, gates, w1, w3, w2, dy):
        td, top = route_idx.shape
        el, dm, fh = w1.shape
        rows = npd * CAP
        aux = jnp.concatenate([route_idx.T.astype(F32), gates.T], axis=0)
        auxa = lax.all_gather(aux, ep, axis=0)
        xa = lax.all_gather(x, ep, axis=0, tiled=True)
        dya = lax.all_gather(dy, ep, axis=0, tiled=True)
        sds = jax.ShapeDtypeStruct
        meta = [pltpu.VMEM((npd, el, td), F32), pltpu.VMEM((npd, el, td), F32)]
        y, u, v, xe = pl.pallas_call(
            functools.partial(_fwd_kernel, npd, td, el),
            grid=(el,),
            in_specs=[_full((npd, 2 * top, td)), _full((npd * td, dm)), _per((dm, fh)), _per((dm, fh)), _per((fh, dm))],
            out_specs=[_full((npd * td, dm)), _per((rows, fh)), _per((rows, fh)), _per((rows, dm))],
            out_shape=[sds((npd * td, dm), F32), sds((el, rows, fh), BF), sds((el, rows, fh), BF), sds((el, rows, dm), BF)],
            scratch_shapes=meta + [pltpu.VMEM((GRP, npd, CAP, dm), BF), pltpu.VMEM((GRP, npd, CAP, dm), BF)],
            name='moe_fwd',
        )(auxa, xa, w1, w3, w2)
        dx, dg, dw2, du, dv = pl.pallas_call(
            functools.partial(_bwd_kernel, npd, td, el),
            grid=(el,),
            in_specs=[_full((npd, 2 * top, td)), _full((npd * td, dm)), _per((rows, fh)), _per((rows, fh)),
                      _per((dm, fh)), _per((dm, fh)), _per((fh, dm))],
            out_specs=[_full((npd * td, dm)), _full((npd, top, td)), _per((fh, dm)), _per((rows, fh)), _per((rows, fh))],
            out_shape=[sds((npd * td, dm), F32), sds((npd, top, td), F32), sds((el, fh, dm), F32),
                       sds((el, rows, fh), BF), sds((el, rows, fh), BF)],
            scratch_shapes=meta + [pltpu.VMEM((GRP, npd, CAP, dm), BF), pltpu.VMEM((GRP, npd, CAP, dm), BF),
                                   pltpu.VMEM((GRP, npd, CAP, 128), F32), pltpu.VMEM((GRP, npd, CAP, 128), F32)],
            name='moe_bwd',
        )(auxa, dya, u, v, w1, w3, w2)
        dw1, dw3 = pl.pallas_call(
            _dw_kernel,
            grid=(el,),
            in_specs=[_per((rows, dm)), _per((rows, fh)), _per((rows, fh))],
            out_specs=[_per((dm, fh)), _per((dm, fh))],
            out_shape=[sds((el, dm, fh), F32), sds((el, dm, fh), F32)],
            name='moe_dw',
        )(xe, du, dv)
        ys = lax.psum_scatter(y, ep, scatter_dimension=0, tiled=True).astype(BF)
        dxs = lax.psum_scatter(dx, ep, scatter_dimension=0, tiled=True).astype(BF)
        dgs = lax.psum_scatter(dg, ep, scatter_dimension=0, tiled=False)
        return ys, dxs, dgs.T, dw1, dw3, dw2

    return jax.shard_map(body, mesh=mesh, in_specs=(tspec, tspec, tspec, wspec, wspec, wspec, tspec), out_specs=(tspec, tspec, tspec, gspec, gspec, gspec), check_vma=False)
```

time: 546 us -> 302 us (0.55)
  Pallas kernels: 0 us -> 212 us
  local copies, waits for them, and re-layouts: 185 us -> 0 us
  matrix products: 157 us -> 0 us
  waiting for transfers between devices: 134 us -> 51.7 us
  other arithmetic: 47.4 us -> 5.39 us
  starting transfers between devices: 17.1 us -> 0.2 us
  blocking collectives: 0 us -> 14.6 us
  between operations: 1.13 us -> 13.8 us
    pallas_call x0 -> x3, Pallas kernels: none -> 212 us  [the longest x1 84.2 us: body(): pl.pallas_call(functools.partial(_bwd_kernel, npd, td, el), grid=(el,), i...]
    dot_general x10 -> x0, matrix products: 157 us -> none  [the longest x1 20.3 us: body(): dw2 = jnp.einsum('erf,erd->efd', act, de, preferred_element_type=f32)]
    all_to_all x4 -> x0, waiting for transfers between devices: 134 us -> none  [the longest x2 107 us: _to_experts(): r = lax.all_to_all(buf.reshape(npd, el * cap, d), ax, 0, 0, tiled=True)]
    gather x3 -> x0, local copies, waits for them, and re-layouts: 44.4 us -> none  [the longest x1 15.7 us: body(): o_slot = _to_sources(o, npd, el, cap, ep)[rows].reshape(td, top, dm)]
    transpose x4 -> x0, local copies, waits for them, and re-layouts: 40.7 us -> none  [the longest x2 21.7 us: _to_sources(): z.reshape(el, npd, cap, d).transpose(1, 0, 2, 3).reshape(npd, el * cap, d)]
    scatter x2 -> x0, local copies, waits for them, and re-layouts: 37.3 us -> none  [the longest x1 29 us: body(): xs = jnp.zeros((ne * cap, dm), bf).at[rows].set(x[tok])]
    reduce_scatter x0 -> x3, waiting for transfers between devices: none -> 32.8 us  [the longest x1 26.6 us: body(): dgs = lax.psum_scatter(dg, ep, scatter_dimension=0, tiled=False)]
    all_to_all x2 -> x0, local copies, waits for them, and re-layouts: 21.8 us -> none  [_to_experts(): r = lax.all_to_all(buf.reshape(npd, el * cap, d), ax, 0, 0, tiled=True)]
  transfers between devices with their start and end apart: 4 -> 5, of which waited for: 4 -> 3; matrix products, arithmetic and copies ran while one was open for 54% -> 2% of each run, Pallas kernels for 0% -> 71%
where the time goes in v1:
time: 302 us; the launch traced here: 298 us
  Pallas kernels  212 us (70%)
  waiting for transfers between devices  51.7 us (17%)
  blocking collectives  14.6 us (5%)
  between operations  13.8 us (5%)
  other arithmetic  5.39 us (2%)
    pallas_call x1, Pallas kernels, body(): pl.pallas_call(functools.partial(_bwd_kernel, npd, td, el), grid=(el,), i...  84.2 us
    pallas_call x1, Pallas kernels, body(): pl.pallas_call(functools.partial(_fwd_kernel, npd, td, el), grid=(el,), i...  78.5 us
    pallas_call x1, Pallas kernels, body(): pl.pallas_call(_dw_kernel, grid=(el,), in_specs=[_per((rows, dm)), _per((...  49.2 us
    reduce_scatter x1, waiting for transfers between devices, body(): dgs = lax.psum_scatter(dg, ep, scatter_dimension=0, tiled=False)  26.6 us
    all_gather x1, waiting for transfers between devices, body(): xa = lax.all_gather(x, ep, axis=0, tiled=True)  16.9 us
    all_gather x1, blocking collectives, body(): auxa = lax.all_gather(aux, ep, axis=0)  14.6 us
    reduce_scatter x1, waiting for transfers between devices, body(): dxs = lax.psum_scatter(dx, ep, scatter_dimension=0, tiled=True).astype(BF)  6.24 us
  transfers between devices with their start and end apart: 5, of which 3 were waited for; matrix products, arithmetic and copies ran while one was open for 2% of the time, Pallas kernels for 71%

profile of v1, /device:TPU:0, one launch (start us, length us, event | category | flops | bytes accessed | tf_op | source)
XLA Modules:
  0.0 297.6 jit_solution(15392010269482160776)
XLA Ops:
  7.2 0.0 all-gather.4.cloned.1.call-start
  7.2 0.7 all-gather.4.cloned.1.call-update
  7.9 0.0 all-gather.6.cloned.1.call-start
  7.9 0.7 all-gather.6.cloned.1.call-update
  8.6 0.0 reduce-scatter.4.cloned.1.call-start
  8.7 0.7 convert_bitcast_fusion
  9.4 0.7 pad_maximum_fusion
  10.1 14.6 %all-gather = f32[128,256]{1,0:T(8,128)} all-gather(f32[16,256]{1,0:T(8,128)S(1)} %pad_maximum_fusion), channel_id=2, replica_groups=mesh['dp'=1,'row'=2,'col'=2,'core'=2] {'row','col','core'}, dimensions={0}, use_global_device_ids=true | all-gather | bytes 147456 | tf_op jit(solution)/shard_map/all_gather | solution.py:207
  24.7 16.9 %all-gather.4.cloned.1.call-done.x_ref = bf16[2048,896]{1,0:T(8,128)(2,1)} async-done(((bf16[256,896]{1,0:T(8,128)(2,1)}), bf16[2048,896]{1,0:T(8,128)(2,1)}) %all-gather.4.cloned.1.call-update) | async-done | bytes 3670032 | tf_op jit(solution)/shard_map/all_gather | solution.py:208
  41.7 78.5 %moe_fwd.1 = (f32[2048,896]{1,0:T(8,128)}, bf16[48,128,256]{2,1,0:T(8,128)(2,1)}, bf16[48,128,256]{2,1,0:T(8,128)(2,1)}, bf16[48,128,896]{2,1,0:T(8,128)(2,1)}) custom-call(f32[8,16,256]{2,1,0:T(8,128)} %bitcast.7, bf16[2048,896]{1,0:T(8,128)(2,1)} %all-gather.4.cloned.1.call-done.x_ref, bf16[48,896,256]{2,1,0:T(8,128)(2,1)} %w1_ref.3, ...), custom_call_target="tpu_custom_call" | custom-call | tf_op jit(solution)/shard_map/moe_fwd/pallas_call | solution.py:212
  120.1 0.0 reduce-scatter.4.cloned.1.call-update
  120.2 0.0 reduce-scatter.6.cloned.1.call-start
  120.2 0.0 all-gather.6.cloned.1.call-done.dy_ref
  120.2 84.2 %moe_bwd.1 = (f32[2048,896]{1,0:T(8,128)}, f32[8,8,256]{2,1,0:T(8,128)}, f32[48,256,896]{2,1,0:T(8,128)}, bf16[48,128,256]{2,1,0:T(8,128)(2,1)}, bf16[48,128,256]{2,1,0:T(8,128)(2,1)}) custom-call(f32[8,16,256]{2,1,0:T(8,128)} %bitcast.8, bf16[2048,896]{1,0:T(8,128)(2,1)} %all-gather.6.cloned.1.call-done.dy_ref, ...), custom_call_target="tpu_custom_call" | custom-call | tf_op jit(solution)/shard_map/moe_bwd/pallas_call | solution.py:221
  204.5 0.0 reduce-scatter.6.cloned.1.call-update
  204.5 0.0 reduce-scatter.8.cloned.1.call-start
  204.5 0.5 reduce-scatter.8.cloned.1.call-update
  205.1 49.2 %moe_dw.1 = (f32[48,896,256]{2,1,0:T(8,128)}, f32[48,896,256]{2,1,0:T(8,128)}) custom-call(bf16[48,128,896]{2,1,0:T(8,128)(2,1)} %get-tuple-element.22.xe_ref, bf16[48,128,256]{2,1,0:T(8,128)(2,1)} %get-tuple-element.23.du_ref, bf16[48,128,256]{2,1,0:T(8,128)(2,1)} %get-tuple-element.24.dv_ref), custom_call_target="tpu_custom_call" | custom-call | tf_op jit(solution)/shard_map/moe_dw/pallas_call | solution.py:233
  254.3 0.0 reduce-scatter.4.cloned.1.call-done
  254.3 2.0 convert_element_type.14
  256.3 6.2 %reduce-scatter.6.cloned.1.call-done = f32[256,896]{1,0:T(8,128)} async-done(((f32[2048,896]{1,0:T(8,128)}), f32[256,896]{1,0:T(8,128)}) %reduce-scatter.6.cloned.1.call-update) | async-done | bytes 917520 | tf_op jit(solution)/shard_map/reduce_scatter | solution.py:242
  262.5 2.0 convert_element_type.15
  264.5 26.6 %reduce-scatter.8.cloned.1.call-done = f32[1,8,256]{2,1,0:T(8,128)} async-done(((f32[8,8,256]{2,1,0:T(8,128)}), f32[1,8,256]{2,1,0:T(8,128)}) %reduce-scatter.8.cloned.1.call-update) | async-done | bytes 8208 | tf_op jit(solution)/shard_map/reduce_scatter | solution.py:243
Async XLA Ops:
  7.2 34.5 %all-gather.4.cloned.1.call-start = ((), (), s32[]{:S(2)}) async-start(), calls=%async_computation.3 | async-start | bytes 4128768 | tf_op jit(solution)/shard_map/all_gather | solution.py:208
  7.9 112.3 %all-gather.6.cloned.1.call-start = ((), (), s32[]{:S(2)}) async-start(), calls=%async_computation.5 | async-start | bytes 4128768 | tf_op jit(solution)/shard_map/all_gather | solution.py:209
  8.6 245.6 %reduce-scatter.4.cloned.1.call-start = ((), (), s32[]{:S(2)}) async-start(), calls=%async_computation.4 | async-start | bytes 8257536 | tf_op jit(solution)/shard_map/reduce_scatter | solution.py:241
  120.2 142.3 %reduce-scatter.6.cloned.1.call-start = ((), (), s32[]{:S(2)}) async-start(), calls=%async_computation.6 | async-start | bytes 8257536 | tf_op jit(solution)/shard_map/reduce_scatter | solution.py:242
  204.5 86.6 %reduce-scatter.8.cloned.1.call-start = ((), (), s32[]{:S(2)}) async-start(), calls=%async_computation.7 | async-start | bytes 73728 | tf_op jit(solution)/shard_map/reduce_scatter | solution.py:243
Sparse Core Ops, SparseCore 0:
  9.8 31.8 all-gather.3
  43.5 28.5 all-gather.5
  120.3 57.8 reduce-scatter.3
  204.6 57.8 reduce-scatter.5
  265.8 25.1 reduce-scatter.7
